TPU v7x, 32 devices: a whole 2x2x4 slice. The times are simulated.
32 devices in a mesh: group: 8 (over z, x), local: 4 (over y, core).
Axes of the slice: x: 2, y: 2, z: 4, core: 2. Of those that a mesh axis runs over, the one named last changes fastest.
Arguments:
- ids: int32 [4096, 32, 8], P(('group', 'local')), may hold values from 0 to 4095
- lengths: int32 [4096, 32], P(('group', 'local')), may hold values from 1 to 8, as said below
- id_weights: float32 [4096, 32, 8], P(('group', 'local')), may hold values from 0.5 to 1.5
- table: float32 [131072, 256], P(('group', 'local')), may hold values from -2.4 to 2.4
Outputs:
- pooled: float32 [4096, 32, 256], P(('group', 'local'))
Inputs may be any that keep to these rules, and one draw needn't show every extreme that they name: `lengths`: every draw has some bag with 8 live ids.
All inputs are finite; a program needn't handle non-finite values.
Results may differ from a plain program's by a relative error of at most 0.00002.
Values sent between devices are 32-bit elements; how exact they have to be, the bound alone decides.
No kernel may reach another device: no remote copies, remote signals or barrier semaphores. Data moves between devices by JAX's collectives and lax.ppermute only.
A program may use at most 128 MiB of HBM per device.

v0:
```python
import jax
import jax.numpy as jnp
from jax import lax
from jax.sharding import PartitionSpec as P


def pool_block(table, pair):
    rows = jnp.take(table, pair[0], axis=0)
    return jnp.sum(rows * pair[1][:, :, None], axis=1)


def partial_pool(table):

    def apply_block(pair):
        return pool_block(table, pair)

    return apply_block


def body(ids, lengths, id_weights, table):
    examples, tables, bag = ids.shape
    n_group = lax.axis_size("group")
    n_local = lax.axis_size("local")
    devices = n_group * n_local
    tab_dev = tables // devices
    rows_each = table.shape[0] // tab_dev
    width = table.shape[1]
    slot = lax.broadcasted_iota(jnp.int32, ids.shape, 2)
    masked = jnp.where(slot < lengths[:, :, None], id_weights, jnp.zeros_like(id_weights))
    packed = jnp.concatenate([ids.astype(jnp.float32), masked], axis=2)
    arrived = lax.all_to_all(packed, ("group", "local"), split_axis=1, concat_axis=0, tiled=True)
    offsets = (jnp.arange(tab_dev, dtype=jnp.int32) * rows_each)[None, :, None]
    index = arrived[:, :, :bag].astype(jnp.int32) + offsets
    weights = arrived[:, :, bag:]
    per_step = max(1, 512 // (examples * tab_dev))
    while devices % per_step:
        per_step = per_step // 2
    blocks = devices // per_step
    block_rows = per_step * examples * tab_dev
    pooled = lax.map(
        partial_pool(table),
        (index.reshape(blocks, block_rows, bag), weights.reshape(blocks, block_rows, bag)),
    )
    pooled = pooled.reshape(devices * examples, tab_dev, width)
    result = lax.all_to_all(pooled, ("group", "local"), split_axis=0, concat_axis=1, tiled=True)
    return result


def solution(mesh):
    placed = (
        P(("group", "local"), None, None),
        P(("group", "local"), None),
        P(("group", "local"), None, None),
        P(("group", "local"), None),
    )
    return jax.shard_map(
        body,
        mesh=mesh,
        in_specs=placed,
        out_specs=P(("group", "local"), None, None),
        check_vma=False,
    )
```

profile of v0, /device:TPU:0, one launch (start us, length us, event | category | flops | bytes accessed | tf_op | source)
XLA Modules:
  0.0 332.3 jit_solution(10436769486742888752)
XLA Ops:
  0.0 0.9 convert_element_type.6
  0.9 0.9 fusion.2
  1.8 0.7 pad_maximum_fusion
  2.6 7.3 %all-to-all-start = ((f32[128,32,16]{0,2,1:T(8,128)}), f32[128,32,16]{0,2,1:T(8,128)S(1)}, u32[]{:S(2)}, u32[]{:S(2)}) async-start(f32[128,32,16]{0,2,1:T(8,128)} %pad_maximum_fusion), calls=%async_computation | async-start | bytes 524288 | tf_op jit(solution)/shard_map/all_to_all | solution.py:31
  9.9 10.6 %all-to-all-done = f32[128,32,16]{0,2,1:T(8,128)S(1)} async-done(((f32[128,32,16]{0,2,1:T(8,128)}), f32[128,32,16]{0,2,1:T(8,128)S(1)}, u32[]{:S(2)}, u32[]{:S(2)}) %all-to-all-start) | async-done | bytes 262176 | tf_op jit(solution)/shard_map/all_to_all | solution.py:31
  20.7 1.9 copy.15
  22.6 0.6 copy.14
  23.2 200.9 %while.10 = (s32[]{:T(128)}, f32[8,512,256]{2,1,0:T(8,128)}, s32[8,512,8]{2,1,0:T(8,128)S(1)}, f32[4096,256]{1,0:T(8,128)}, f32[8,512,8]{2,1,0:T(8,128)}, /*index=5*/s32[]{:T(128)}) while((s32[]{:T(128)}, f32[8,512,256]{2,1,0:T(8,128)}, s32[8,512,8]{2,1,0:T(8,128)S(1)}, f32[4096,256]{1,0:T(8,128)}, f32[8,512,8]{2,1,0:T(8,128)}, ...), condition=%wide.region_2.3_spmd, body=%wide.region_0.2_spmd.sunk | while | flops 3055618 | bytes 14344785 | solution.py:40
  23.3 0.1 reshape.63
  23.4 18.3 %gather_fusion = f32[4096,256]{1,0:T(8,128)} fusion(f32[4096,256]{1,0:T(8,128)} %get-tuple-element.101, s32[4096]{0:T(1024)S(1)} %broadcast_clamp_fusion.2), kind=kCustom, calls=%fused_computation.clone.1 | custom fusion | bytes 8404992 | tf_op jit(solution)/shard_map/while/body/eval_jaxpr/jit(_take)/gather | solution.py:8
  41.8 1.0 dynamic-slice_bitcast_fusion.2
  42.8 4.7 %fusion.5 = f32[512,256]{1,0:T(8,128)S(1)} fusion(f32[4096,256]{1,0:T(8,128)} %gather_fusion, f32[512,8]{1,0:T(8,128)S(1)} %dynamic-slice_bitcast_fusion.2, pred[512,8]{1,0:T(8,128)(4,1)S(1)} %compare_and_fusion.2), kind=kLoop, calls=%fused_computation.3.clone.1 | loop fusion | flops 3014656 | bytes 4739072 | tf_op jit(solution)/shard_map/while/body/eval_jaxpr/reduce_sum | solution.py:9
  47.5 0.8 bitcast_dynamic-update-slice_fusion.2
  48.4 0.1 reshape.63
  48.5 18.3 %gather_fusion = f32[4096,256]{1,0:T(8,128)} fusion(f32[4096,256]{1,0:T(8,128)} %get-tuple-element.101, s32[4096]{0:T(1024)S(1)} %broadcast_clamp_fusion.2), kind=kCustom, calls=%fused_computation.clone.1 | custom fusion | bytes 8404992 | tf_op jit(solution)/shard_map/while/body/eval_jaxpr/jit(_take)/gather | solution.py:8
  66.9 1.0 dynamic-slice_bitcast_fusion.2
  67.9 4.7 %fusion.5 = f32[512,256]{1,0:T(8,128)S(1)} fusion(f32[4096,256]{1,0:T(8,128)} %gather_fusion, f32[512,8]{1,0:T(8,128)S(1)} %dynamic-slice_bitcast_fusion.2, pred[512,8]{1,0:T(8,128)(4,1)S(1)} %compare_and_fusion.2), kind=kLoop, calls=%fused_computation.3.clone.1 | loop fusion | flops 3014656 | bytes 4739072 | tf_op jit(solution)/shard_map/while/body/eval_jaxpr/reduce_sum | solution.py:9
  72.6 0.8 bitcast_dynamic-update-slice_fusion.2
  73.5 0.1 reshape.63
  73.6 18.3 %gather_fusion = f32[4096,256]{1,0:T(8,128)} fusion(f32[4096,256]{1,0:T(8,128)} %get-tuple-element.101, s32[4096]{0:T(1024)S(1)} %broadcast_clamp_fusion.2), kind=kCustom, calls=%fused_computation.clone.1 | custom fusion | bytes 8404992 | tf_op jit(solution)/shard_map/while/body/eval_jaxpr/jit(_take)/gather | solution.py:8
  92.0 1.0 dynamic-slice_bitcast_fusion.2
  93.0 4.7 %fusion.5 = f32[512,256]{1,0:T(8,128)S(1)} fusion(f32[4096,256]{1,0:T(8,128)} %gather_fusion, f32[512,8]{1,0:T(8,128)S(1)} %dynamic-slice_bitcast_fusion.2, pred[512,8]{1,0:T(8,128)(4,1)S(1)} %compare_and_fusion.2), kind=kLoop, calls=%fused_computation.3.clone.1 | loop fusion | flops 3014656 | bytes 4739072 | tf_op jit(solution)/shard_map/while/body/eval_jaxpr/reduce_sum | solution.py:9
  97.7 0.8 bitcast_dynamic-update-slice_fusion.2
  98.8 18.3 %gather_fusion = f32[4096,256]{1,0:T(8,128)} fusion(f32[4096,256]{1,0:T(8,128)} %get-tuple-element.101, s32[4096]{0:T(1024)S(1)} %broadcast_clamp_fusion.2), kind=kCustom, calls=%fused_computation.clone.1 | custom fusion | bytes 8404992 | tf_op jit(solution)/shard_map/while/body/eval_jaxpr/jit(_take)/gather | solution.py:8
  117.1 1.0 dynamic-slice_bitcast_fusion.2
  118.1 4.7 %fusion.5 = f32[512,256]{1,0:T(8,128)S(1)} fusion(f32[4096,256]{1,0:T(8,128)} %gather_fusion, f32[512,8]{1,0:T(8,128)S(1)} %dynamic-slice_bitcast_fusion.2, pred[512,8]{1,0:T(8,128)(4,1)S(1)} %compare_and_fusion.2), kind=kLoop, calls=%fused_computation.3.clone.1 | loop fusion | flops 3014656 | bytes 4739072 | tf_op jit(solution)/shard_map/while/body/eval_jaxpr/reduce_sum | solution.py:9
  122.8 0.8 bitcast_dynamic-update-slice_fusion.2
  123.9 18.3 %gather_fusion = f32[4096,256]{1,0:T(8,128)} fusion(f32[4096,256]{1,0:T(8,128)} %get-tuple-element.101, s32[4096]{0:T(1024)S(1)} %broadcast_clamp_fusion.2), kind=kCustom, calls=%fused_computation.clone.1 | custom fusion | bytes 8404992 | tf_op jit(solution)/shard_map/while/body/eval_jaxpr/jit(_take)/gather | solution.py:8
  142.2 1.0 dynamic-slice_bitcast_fusion.2
  143.2 4.7 %fusion.5 = f32[512,256]{1,0:T(8,128)S(1)} fusion(f32[4096,256]{1,0:T(8,128)} %gather_fusion, f32[512,8]{1,0:T(8,128)S(1)} %dynamic-slice_bitcast_fusion.2, pred[512,8]{1,0:T(8,128)(4,1)S(1)} %compare_and_fusion.2), kind=kLoop, calls=%fused_computation.3.clone.1 | loop fusion | flops 3014656 | bytes 4739072 | tf_op jit(solution)/shard_map/while/body/eval_jaxpr/reduce_sum | solution.py:9
  147.9 0.8 bitcast_dynamic-update-slice_fusion.2
  148.8 0.1 reshape.63
  149.0 18.3 %gather_fusion = f32[4096,256]{1,0:T(8,128)} fusion(f32[4096,256]{1,0:T(8,128)} %get-tuple-element.101, s32[4096]{0:T(1024)S(1)} %broadcast_clamp_fusion.2), kind=kCustom, calls=%fused_computation.clone.1 | custom fusion | bytes 8404992 | tf_op jit(solution)/shard_map/while/body/eval_jaxpr/jit(_take)/gather | solution.py:8
  167.3 1.0 dynamic-slice_bitcast_fusion.2
  168.3 4.7 %fusion.5 = f32[512,256]{1,0:T(8,128)S(1)} fusion(f32[4096,256]{1,0:T(8,128)} %gather_fusion, f32[512,8]{1,0:T(8,128)S(1)} %dynamic-slice_bitcast_fusion.2, pred[512,8]{1,0:T(8,128)(4,1)S(1)} %compare_and_fusion.2), kind=kLoop, calls=%fused_computation.3.clone.1 | loop fusion | flops 3014656 | bytes 4739072 | tf_op jit(solution)/shard_map/while/body/eval_jaxpr/reduce_sum | solution.py:9
  173.0 0.8 bitcast_dynamic-update-slice_fusion.2
  174.1 18.3 %gather_fusion = f32[4096,256]{1,0:T(8,128)} fusion(f32[4096,256]{1,0:T(8,128)} %get-tuple-element.101, s32[4096]{0:T(1024)S(1)} %broadcast_clamp_fusion.2), kind=kCustom, calls=%fused_computation.clone.1 | custom fusion | bytes 8404992 | tf_op jit(solution)/shard_map/while/body/eval_jaxpr/jit(_take)/gather | solution.py:8
  192.4 1.0 dynamic-slice_bitcast_fusion.2
  193.4 4.7 %fusion.5 = f32[512,256]{1,0:T(8,128)S(1)} fusion(f32[4096,256]{1,0:T(8,128)} %gather_fusion, f32[512,8]{1,0:T(8,128)S(1)} %dynamic-slice_bitcast_fusion.2, pred[512,8]{1,0:T(8,128)(4,1)S(1)} %compare_and_fusion.2), kind=kLoop, calls=%fused_computation.3.clone.1 | loop fusion | flops 3014656 | bytes 4739072 | tf_op jit(solution)/shard_map/while/body/eval_jaxpr/reduce_sum | solution.py:9
  198.2 0.8 bitcast_dynamic-update-slice_fusion.2
  199.2 18.3 %gather_fusion = f32[4096,256]{1,0:T(8,128)} fusion(f32[4096,256]{1,0:T(8,128)} %get-tuple-element.101, s32[4096]{0:T(1024)S(1)} %broadcast_clamp_fusion.2), kind=kCustom, calls=%fused_computation.clone.1 | custom fusion | bytes 8404992 | tf_op jit(solution)/shard_map/while/body/eval_jaxpr/jit(_take)/gather | solution.py:8
  217.5 1.0 dynamic-slice_bitcast_fusion.2
  218.5 4.7 %fusion.5 = f32[512,256]{1,0:T(8,128)S(1)} fusion(f32[4096,256]{1,0:T(8,128)} %gather_fusion, f32[512,8]{1,0:T(8,128)S(1)} %dynamic-slice_bitcast_fusion.2, pred[512,8]{1,0:T(8,128)(4,1)S(1)} %compare_and_fusion.2), kind=kLoop, calls=%fused_computation.3.clone.1 | loop fusion | flops 3014656 | bytes 4739072 | tf_op jit(solution)/shard_map/while/body/eval_jaxpr/reduce_sum | solution.py:9
  223.3 0.8 bitcast_dynamic-update-slice_fusion.2
  224.1 7.1 %reshape.48 = f32[4096,1,256]{2,1,0:T(1,128)} reshape(f32[8,512,256]{2,1,0:T(8,128)} %get-tuple-element.32) | data formatting | bytes 8388608 | tf_op jit(solution)/shard_map/reshape | solution.py:44
  231.2 96.4 %all_to_all.36 = f32[4096,1,256]{2,1,0:T(1,128)S(1)} all-to-all(f32[4096,1,256]{2,1,0:T(1,128)} %reshape.48), channel_id=1, replica_groups=mesh['group'=8,'local'=4] {'group','local'}, dimensions={0} | all-to-all | bytes 8388608 | tf_op jit(solution)/shard_map/all_to_all | solution.py:45
  327.6 0.3 copy.16
  327.9 4.4 %copy.13 = f32[128,32,256]{2,1,0:T(8,128)} copy(f32[128,32,256]{2,0,1:T(8,128)S(1)} %bitcast.40) | data formatting | bytes 8388608 | tf_op jit(solution)/shard_map/all_to_all | solution.py:45
  (31 shorter events, 1.7 us)
Async XLA Ops:
  2.6 17.9 %all-to-all-start = ((f32[128,32,16]{0,2,1:T(8,128)}), f32[128,32,16]{0,2,1:T(8,128)S(1)}, u32[]{:S(2)}, u32[]{:S(2)}) async-start(f32[128,32,16]{0,2,1:T(8,128)} %pad_maximum_fusion), calls=%async_computation | async-start | bytes 524288 | tf_op jit(solution)/shard_map/all_to_all | solution.py:31
where the time goes:
time: 334 us; the launch traced here: 332 us
  local copies, waits for them, and re-layouts  176 us (53%)
  blocking collectives  96.4 us (29%)
  other arithmetic  41.6 us (12%)
  waiting for transfers between devices  10.6 us (3%)
  starting transfers between devices  7.33 us (2%)
    gather x8, local copies, waits for them, and re-layouts, pool_block(): rows = jnp.take(table, pair[0], axis=0)  146 us
    all_to_all x1, blocking collectives, body(): lax.all_to_all(pooled, ('group', 'local'), split_axis=0, concat_axis=1, t...  96.4 us
    reduce_sum x8, other arithmetic, pool_block(): return jnp.sum(rows * pair[1][:, :, None], axis=1)  38 us
    all_to_all x1, waiting for transfers between devices, body(): lax.all_to_all(packed, ('group', 'local'), split_axis=1, concat_axis=0, t...  10.6 us
    mul x8, local copies, waits for them, and re-layouts, pool_block(): return jnp.sum(rows * pair[1][:, :, None], axis=1)  7.79 us
    all_to_all x1, starting transfers between devices, body(): lax.all_to_all(packed, ('group', 'local'), split_axis=1, concat_axis=0, t...  7.33 us
    reshape x1, local copies, waits for them, and re-layouts, body(): pooled = pooled.reshape(devices * examples, tab_dev, width)  7.09 us
  transfers between devices with their start and end apart: 1, of which 1 were waited for; matrix products, arithmetic and copies ran while one was open for 0% of the time, Pallas kernels for 0%

commit v1 on v0

--- a/solution.py
+++ b/solution.py
@@ -42,7 +42,10 @@
         (index.reshape(blocks, block_rows, bag), weights.reshape(blocks, block_rows, bag)),
     )
     pooled = pooled.reshape(devices * examples, tab_dev, width)
-    result = lax.all_to_all(pooled, ("group", "local"), split_axis=0, concat_axis=1, tiled=True)
+    n_dev = lax.axis_size(("group", "local"))
+    pieces = jnp.stack(jnp.split(pooled, n_dev, axis=0), axis=0)
+    pieces = lax.all_to_all(pieces, ("group", "local"), split_axis=0, concat_axis=0)
+    result = jnp.concatenate(pieces, axis=1)
     return result
 
 

time: 334 us -> 356 us (1.066)
  local copies, waits for them, and re-layouts: 176 us -> 198 us
    unnamed x1 -> x31, local copies, waits for them, and re-layouts: 0.27 us -> 28.4 us
    all_to_all x1 -> x0, local copies, waits for them, and re-layouts: 4.44 us -> none  [body(): lax.all_to_all(pooled, ('group', 'local'), split_axis=0, concat_axis=1, t...]
where the time goes in v1:
time: 356 us; the launch traced here: 354 us
  local copies, waits for them, and re-layouts  198 us (56%)
  blocking collectives  95.8 us (27%)
  other arithmetic  41.6 us (12%)
  waiting for transfers between devices  10.6 us (3%)
  starting transfers between devices  7.33 us (2%)
    gather x8, local copies, waits for them, and re-layouts, pool_block(): rows = jnp.take(table, pair[0], axis=0)  146 us
    all_to_all x1, blocking collectives, body(): lax.all_to_all(pieces, ('group', 'local'), split_axis=0, concat_axis=0)  95.8 us
    reduce_sum x8, other arithmetic, pool_block(): return jnp.sum(rows * pair[1][:, :, None], axis=1)  38 us
    unnamed x31, local copies, waits for them, and re-layouts  28.4 us
    all_to_all x1, waiting for transfers between devices, body(): lax.all_to_all(packed, ('group', 'local'), split_axis=1, concat_axis=0, t...  10.6 us
    mul x8, local copies, waits for them, and re-layouts, pool_block(): return jnp.sum(rows * pair[1][:, :, None], axis=1)  7.79 us
    all_to_all x1, starting transfers between devices, body(): lax.all_to_all(packed, ('group', 'local'), split_axis=1, concat_axis=0, t...  7.33 us
  transfers between devices with their start and end apart: 1, of which 1 were waited for; matrix products, arithmetic and copies ran while one was open for 0% of the time, Pallas kernels for 0%

profile of v1, /device:TPU:0, one launch (start us, length us, event | category | flops | bytes accessed | tf_op | source)
XLA Modules:
  0.0 353.8 jit_solution(16742254887787897076)
XLA Ops:
  0.9 0.9 fusion.34
  2.6 7.3 %all-to-all-start = ((f32[128,32,16]{0,2,1:T(8,128)}), f32[128,32,16]{0,2,1:T(8,128)S(1)}, u32[]{:S(2)}, u32[]{:S(2)}) async-start(f32[128,32,16]{0,2,1:T(8,128)} %pad_maximum_fusion), calls=%async_computation | async-start | bytes 524288 | tf_op jit(solution)/shard_map/all_to_all | solution.py:31
  9.9 10.6 %all-to-all-done = f32[128,32,16]{0,2,1:T(8,128)S(1)} async-done(((f32[128,32,16]{0,2,1:T(8,128)}), f32[128,32,16]{0,2,1:T(8,128)S(1)}, u32[]{:S(2)}, u32[]{:S(2)}) %all-to-all-start) | async-done | bytes 262176 | tf_op jit(solution)/shard_map/all_to_all | solution.py:31
  20.7 1.9 copy.76
  23.2 200.9 %while.10 = (s32[]{:T(128)}, f32[8,512,256]{2,1,0:T(8,128)}, s32[8,512,8]{2,1,0:T(8,128)S(1)}, f32[4096,256]{1,0:T(8,128)}, f32[8,512,8]{2,1,0:T(8,128)}, /*index=5*/s32[]{:T(128)}) while((s32[]{:T(128)}, f32[8,512,256]{2,1,0:T(8,128)}, s32[8,512,8]{2,1,0:T(8,128)S(1)}, f32[4096,256]{1,0:T(8,128)}, f32[8,512,8]{2,1,0:T(8,128)}, ...), condition=%wide.region_2.3_spmd, body=%wide.region_0.2_spmd.sunk | while | flops 3055618 | bytes 14344785 | solution.py:40
  23.4 18.3 %gather_fusion = f32[4096,256]{1,0:T(8,128)} fusion(f32[4096,256]{1,0:T(8,128)} %get-tuple-element.101, s32[4096]{0:T(1024)S(1)} %broadcast_clamp_fusion.2), kind=kCustom, calls=%fused_computation.clone.1 | custom fusion | bytes 8404992 | tf_op jit(solution)/shard_map/while/body/eval_jaxpr/jit(_take)/gather | solution.py:8
  41.8 1.0 dynamic-slice_bitcast_fusion.2
  42.8 4.7 %fusion.37 = f32[512,256]{1,0:T(8,128)S(1)} fusion(f32[4096,256]{1,0:T(8,128)} %gather_fusion, f32[512,8]{1,0:T(8,128)S(1)} %dynamic-slice_bitcast_fusion.2, pred[512,8]{1,0:T(8,128)(4,1)S(1)} %compare_and_fusion.2), kind=kLoop, calls=%fused_computation.3.clone.1 | loop fusion | flops 3014656 | bytes 4739072 | tf_op jit(solution)/shard_map/while/body/eval_jaxpr/reduce_sum | solution.py:9
  48.5 18.3 %gather_fusion = f32[4096,256]{1,0:T(8,128)} fusion(f32[4096,256]{1,0:T(8,128)} %get-tuple-element.101, s32[4096]{0:T(1024)S(1)} %broadcast_clamp_fusion.2), kind=kCustom, calls=%fused_computation.clone.1 | custom fusion | bytes 8404992 | tf_op jit(solution)/shard_map/while/body/eval_jaxpr/jit(_take)/gather | solution.py:8
  66.9 1.0 dynamic-slice_bitcast_fusion.2
  67.9 4.7 %fusion.37 = f32[512,256]{1,0:T(8,128)S(1)} fusion(f32[4096,256]{1,0:T(8,128)} %gather_fusion, f32[512,8]{1,0:T(8,128)S(1)} %dynamic-slice_bitcast_fusion.2, pred[512,8]{1,0:T(8,128)(4,1)S(1)} %compare_and_fusion.2), kind=kLoop, calls=%fused_computation.3.clone.1 | loop fusion | flops 3014656 | bytes 4739072 | tf_op jit(solution)/shard_map/while/body/eval_jaxpr/reduce_sum | solution.py:9
  73.6 18.3 %gather_fusion = f32[4096,256]{1,0:T(8,128)} fusion(f32[4096,256]{1,0:T(8,128)} %get-tuple-element.101, s32[4096]{0:T(1024)S(1)} %broadcast_clamp_fusion.2), kind=kCustom, calls=%fused_computation.clone.1 | custom fusion | bytes 8404992 | tf_op jit(solution)/shard_map/while/body/eval_jaxpr/jit(_take)/gather | solution.py:8
  92.0 1.0 dynamic-slice_bitcast_fusion.2
  93.0 4.7 %fusion.37 = f32[512,256]{1,0:T(8,128)S(1)} fusion(f32[4096,256]{1,0:T(8,128)} %gather_fusion, f32[512,8]{1,0:T(8,128)S(1)} %dynamic-slice_bitcast_fusion.2, pred[512,8]{1,0:T(8,128)(4,1)S(1)} %compare_and_fusion.2), kind=kLoop, calls=%fused_computation.3.clone.1 | loop fusion | flops 3014656 | bytes 4739072 | tf_op jit(solution)/shard_map/while/body/eval_jaxpr/reduce_sum | solution.py:9
  98.8 18.3 %gather_fusion = f32[4096,256]{1,0:T(8,128)} fusion(f32[4096,256]{1,0:T(8,128)} %get-tuple-element.101, s32[4096]{0:T(1024)S(1)} %broadcast_clamp_fusion.2), kind=kCustom, calls=%fused_computation.clone.1 | custom fusion | bytes 8404992 | tf_op jit(solution)/shard_map/while/body/eval_jaxpr/jit(_take)/gather | solution.py:8
  117.1 1.0 dynamic-slice_bitcast_fusion.2
  118.1 4.7 %fusion.37 = f32[512,256]{1,0:T(8,128)S(1)} fusion(f32[4096,256]{1,0:T(8,128)} %gather_fusion, f32[512,8]{1,0:T(8,128)S(1)} %dynamic-slice_bitcast_fusion.2, pred[512,8]{1,0:T(8,128)(4,1)S(1)} %compare_and_fusion.2), kind=kLoop, calls=%fused_computation.3.clone.1 | loop fusion | flops 3014656 | bytes 4739072 | tf_op jit(solution)/shard_map/while/body/eval_jaxpr/reduce_sum | solution.py:9
  123.9 18.3 %gather_fusion = f32[4096,256]{1,0:T(8,128)} fusion(f32[4096,256]{1,0:T(8,128)} %get-tuple-element.101, s32[4096]{0:T(1024)S(1)} %broadcast_clamp_fusion.2), kind=kCustom, calls=%fused_computation.clone.1 | custom fusion | bytes 8404992 | tf_op jit(solution)/shard_map/while/body/eval_jaxpr/jit(_take)/gather | solution.py:8
  142.2 1.0 dynamic-slice_bitcast_fusion.2
  143.2 4.7 %fusion.37 = f32[512,256]{1,0:T(8,128)S(1)} fusion(f32[4096,256]{1,0:T(8,128)} %gather_fusion, f32[512,8]{1,0:T(8,128)S(1)} %dynamic-slice_bitcast_fusion.2, pred[512,8]{1,0:T(8,128)(4,1)S(1)} %compare_and_fusion.2), kind=kLoop, calls=%fused_computation.3.clone.1 | loop fusion | flops 3014656 | bytes 4739072 | tf_op jit(solution)/shard_map/while/body/eval_jaxpr/reduce_sum | solution.py:9
  149.0 18.3 %gather_fusion = f32[4096,256]{1,0:T(8,128)} fusion(f32[4096,256]{1,0:T(8,128)} %get-tuple-element.101, s32[4096]{0:T(1024)S(1)} %broadcast_clamp_fusion.2), kind=kCustom, calls=%fused_computation.clone.1 | custom fusion | bytes 8404992 | tf_op jit(solution)/shard_map/while/body/eval_jaxpr/jit(_take)/gather | solution.py:8
  167.3 1.0 dynamic-slice_bitcast_fusion.2
  168.3 4.7 %fusion.37 = f32[512,256]{1,0:T(8,128)S(1)} fusion(f32[4096,256]{1,0:T(8,128)} %gather_fusion, f32[512,8]{1,0:T(8,128)S(1)} %dynamic-slice_bitcast_fusion.2, pred[512,8]{1,0:T(8,128)(4,1)S(1)} %compare_and_fusion.2), kind=kLoop, calls=%fused_computation.3.clone.1 | loop fusion | flops 3014656 | bytes 4739072 | tf_op jit(solution)/shard_map/while/body/eval_jaxpr/reduce_sum | solution.py:9
  174.1 18.3 %gather_fusion = f32[4096,256]{1,0:T(8,128)} fusion(f32[4096,256]{1,0:T(8,128)} %get-tuple-element.101, s32[4096]{0:T(1024)S(1)} %broadcast_clamp_fusion.2), kind=kCustom, calls=%fused_computation.clone.1 | custom fusion | bytes 8404992 | tf_op jit(solution)/shard_map/while/body/eval_jaxpr/jit(_take)/gather | solution.py:8
  192.4 1.0 dynamic-slice_bitcast_fusion.2
  193.4 4.7 %fusion.37 = f32[512,256]{1,0:T(8,128)S(1)} fusion(f32[4096,256]{1,0:T(8,128)} %gather_fusion, f32[512,8]{1,0:T(8,128)S(1)} %dynamic-slice_bitcast_fusion.2, pred[512,8]{1,0:T(8,128)(4,1)S(1)} %compare_and_fusion.2), kind=kLoop, calls=%fused_computation.3.clone.1 | loop fusion | flops 3014656 | bytes 4739072 | tf_op jit(solution)/shard_map/while/body/eval_jaxpr/reduce_sum | solution.py:9
  199.2 18.3 %gather_fusion = f32[4096,256]{1,0:T(8,128)} fusion(f32[4096,256]{1,0:T(8,128)} %get-tuple-element.101, s32[4096]{0:T(1024)S(1)} %broadcast_clamp_fusion.2), kind=kCustom, calls=%fused_computation.clone.1 | custom fusion | bytes 8404992 | tf_op jit(solution)/shard_map/while/body/eval_jaxpr/jit(_take)/gather | solution.py:8
  217.5 1.0 dynamic-slice_bitcast_fusion.2
  218.5 4.7 %fusion.37 = f32[512,256]{1,0:T(8,128)S(1)} fusion(f32[4096,256]{1,0:T(8,128)} %gather_fusion, f32[512,8]{1,0:T(8,128)S(1)} %dynamic-slice_bitcast_fusion.2, pred[512,8]{1,0:T(8,128)(4,1)S(1)} %compare_and_fusion.2), kind=kLoop, calls=%fused_computation.3.clone.1 | loop fusion | flops 3014656 | bytes 4739072 | tf_op jit(solution)/shard_map/while/body/eval_jaxpr/reduce_sum | solution.py:9
  225.0 0.9 fusion.32
  225.9 0.9 fusion.31
  226.9 0.9 fusion.30
  227.8 0.9 fusion.29
  228.7 0.9 fusion.28
  229.6 0.9 fusion.27
  230.5 0.9 fusion.26
  232.4 0.9 fusion.24
  235.1 0.9 fusion.21
  237.9 0.9 fusion.18
  240.7 0.9 fusion.15
  243.4 0.9 fusion.12
  244.3 0.9 fusion.11
  246.2 0.9 fusion.9
  247.1 0.9 fusion.8
  249.9 0.9 fusion.5
  252.6 0.9 fusion.2
  253.5 95.8 %all_to_all.23 = f32[32,128,1,256]{3,1,2,0:T(8,128)S(1)} all-to-all(f32[32,128,1,256]{3,1,2,0:T(8,128)S(1)} %fusion.2), channel_id=1, replica_groups=mesh['group'=8,'local'=4] {'group','local'}, dimensions={0} | all-to-all | bytes 8388608 | tf_op jit(solution)/shard_map/all_to_all | solution.py:47
  349.4 4.4 %copy.74 = f32[128,32,256]{2,1,0:T(8,128)} copy(f32[128,32,256]{2,0,1:T(8,128)S(1)} %bitcast.167) | data formatting | bytes 8388608 | tf_op jit(solution)/shard_map/reshape | solution.py:48
  (61 shorter events, 25.0 us)
Async XLA Ops:
  2.6 17.9 %all-to-all-start = ((f32[128,32,16]{0,2,1:T(8,128)}), f32[128,32,16]{0,2,1:T(8,128)S(1)}, u32[]{:S(2)}, u32[]{:S(2)}) async-start(f32[128,32,16]{0,2,1:T(8,128)} %pad_maximum_fusion), calls=%async_computation | async-start | bytes 524288 | tf_op jit(solution)/shard_map/all_to_all | solution.py:31
